TPU v7x, 128 devices: a whole 4x4x4 slice. The times are simulated.
128 devices in a mesh: dp: 16 (over y, x), expert: 4 (over z), tensor: 2 (over core).
Axes of the slice: x: 4, y: 4, z: 4, core: 2. Of those that a mesh axis runs over, the one named last changes fastest.
Arguments:
- tokens: bfloat16 [8192, 2048], P(('dp', 'expert'), 'tensor'), may hold values from -6 to 6
- norm_gain: bfloat16 [2048], replicated, may hold values from 0.25 to 1.75
- expert_ids: int32 [8192, 2], P(('dp', 'expert')), may hold values from 0 to 3, all different within a row; in each aligned block of 128 rows (0 to 127, 128 to 255, ...) at most 128 rows name the same one
- gate_codes: int32 [8192, 2], P(('dp', 'expert')), may hold values from 1 to 255
- gate_weights: bfloat16 [4, 7168, 2048], P('expert', ('dp', 'tensor')), may hold values from -0.125 to 0.125
- up_weights: bfloat16 [4, 7168, 2048], P('expert', ('dp', 'tensor')), may hold values from -0.125 to 0.125
- down_weights: bfloat16 [4, 7168, 2048], P('expert', ('dp', 'tensor')), may hold values from -0.0625 to 0.0625
- value_head: bfloat16 [2048, 128], replicated, may hold values from -0.125 to 0.125
- actions: int32 [8192], P(('dp', 'expert')), may hold values from 0 to 127
- rewards: int32 [8192], P(('dp', 'expert')), may hold values from -8 to 8
- trace_codes: int32 [8192], P(('dp', 'expert')), may hold values from 1 to 1024
Outputs:
- action_values: float32 [8192, 128], P(('dp', 'expert'))
- retrace_targets: float32 [8192], P(('dp', 'expert'))
Inputs may be any that keep to these rules, and one draw needn't show every extreme that they name: `expert_ids`: each row names 2 different experts; within the 128 rows of one index pair of dp and expert each expert is named by at most 128 rows, and in some of these blocks one expert by exactly 128.
All inputs are finite; a program needn't handle non-finite values.
Results may differ from a plain program's by a relative error of at most 0.005.
Values may be sent and summed in bfloat16 or wider, within the bound.
A program may use at most 256 MiB of HBM per device.

v0:
```python
import jax
import jax.numpy as jnp
from jax import lax
from jax.sharding import PartitionSpec as P

STEPS = 128
DISCOUNT = 0.99
EPSILON = 1e-05
HIGHEST = lax.Precision.HIGHEST


def retrace(action_values, actions, rewards, trace_codes):
    greedy = jnp.max(action_values, axis=1)
    picked = (
        actions[:, None] == jnp.arange(action_values.shape[1], dtype=jnp.int32)[None, :]
    ).astype(jnp.float32)
    taken = jnp.sum(action_values * picked, axis=1)
    trace = trace_codes.astype(jnp.float32) / 1024.0
    reward = rewards.astype(jnp.float32) * 0.25
    greedy = greedy.reshape(-1, STEPS)
    taken = taken.reshape(-1, STEPS)
    trace = trace.reshape(-1, STEPS)
    reward = reward.reshape(-1, STEPS)
    padding = jnp.zeros_like(greedy[:, :1])
    greedy_next = jnp.concatenate([greedy[:, 1:], padding], axis=1)
    taken_next = jnp.concatenate([taken[:, 1:], padding], axis=1)
    trace_next = jnp.concatenate([trace[:, 1:], padding], axis=1)
    driver = reward + DISCOUNT * (greedy_next - trace_next * taken_next)
    log_sums = jnp.cumsum(jnp.log(DISCOUNT * trace), axis=1)
    spans = log_sums[:, None, :] - log_sums[:, :, None]
    upper_mask = (
        jnp.arange(STEPS, dtype=jnp.int32)[None, :] >= jnp.arange(STEPS, dtype=jnp.int32)[:, None]
    )
    weight = jnp.where(upper_mask[None, :, :], jnp.exp(jnp.minimum(spans, 0.0)), 0.0)
    target = jnp.einsum("nts,ns->nt", weight, driver, precision=HIGHEST)
    return target.reshape(-1)


def rows_by(a, b):
    return lax.dot_general(a, b, (((1,), (1,)), ((), ())), preferred_element_type=jnp.float32)


def per_device(
    tokens,
    norm_gain,
    expert_ids,
    gate_codes,
    gate_weights,
    up_weights,
    down_weights,
    value_head,
    actions,
    rewards,
    trace_codes,
):
    dp, ex = (lax.axis_size("dp"), lax.axis_size("expert"))
    tp = lax.axis_size("tensor")
    rows, half = tokens.shape
    folded = jnp.dot(down_weights[0], value_head, preferred_element_type=jnp.float32)
    folded = folded.astype(jnp.bfloat16)
    wide = tokens.astype(jnp.float32)
    square = lax.psum(jnp.sum(wide * wide, axis=1, keepdims=True), "tensor") / (half * tp)
    gain = lax.dynamic_slice_in_dim(norm_gain, lax.axis_index("tensor") * half, half)
    normed = wide * lax.rsqrt(square + EPSILON) * gain.astype(jnp.float32)[None, :]
    normed = normed.astype(jnp.bfloat16)
    everyone = lax.all_gather(normed, ("dp", "expert", "tensor"), axis=0)
    everyone = everyone.reshape(dp * ex, tp, rows, half)
    left = everyone[:, 0].reshape(dp * ex * rows, half)
    right = everyone[:, 1].reshape(dp * ex * rows, half)
    gate_m, up_m = (gate_weights[0], up_weights[0])
    gate = rows_by(left, gate_m[:, :half]) + rows_by(right, gate_m[:, half:])
    lift = rows_by(left, up_m[:, :half]) + rows_by(right, up_m[:, half:])
    hidden = (jax.nn.silu(gate) * lift).astype(jnp.bfloat16)
    value = jnp.dot(hidden, folded, preferred_element_type=jnp.float32)
    value = lax.psum_scatter(value, "dp", scatter_dimension=0, tiled=True)
    value = value.reshape(ex, rows, value.shape[1])
    value = lax.all_to_all(value, "expert", split_axis=0, concat_axis=0, tiled=True)
    codes = gate_codes.astype(jnp.float32)
    share = codes / jnp.sum(codes, axis=1, keepdims=True)
    named = expert_ids[None] == jnp.arange(ex, dtype=jnp.int32)[:, None, None]
    by_expert = jnp.sum(jnp.where(named, share[None], 0.0), axis=2)
    blended = jnp.sum(value * by_expert[:, :, None], axis=0)
    action_values = lax.psum(blended, "tensor")
    return (action_values, retrace(action_values, actions, rewards, trace_codes))


def solution(mesh):
    group, weight = (P(("dp", "expert"), None), P("expert", ("dp", "tensor"), None))
    line = P(("dp", "expert"))
    in_specs = (
        P(("dp", "expert"), "tensor"),
        P(),
        group,
        group,
        weight,
        weight,
        weight,
        P(),
        line,
        line,
        line,
    )
    return jax.shard_map(
        per_device, mesh=mesh, in_specs=in_specs, out_specs=(group, line), check_vma=False
    )
```

profile of v0, /device:TPU:1, one launch (start us, length us, event | category | flops | bytes accessed | tf_op | source)
XLA Modules:
  0.0 304.3 jit_solution(3037245187421249182)
XLA Ops:
  7.2 1.2 fusion.4
  8.4 3.5 %psum.14 = f32[128,1]{0,1:T(1,128)S(1)} all-reduce(f32[128,1]{0,1:T(1,128)S(1)} %bitcast.47), channel_id=1, replica_groups=mesh['dp'=16,'expert'=4,'tensor'=2] {'tensor'}, use_global_device_ids=true, to_apply=%region_1.0 | all-reduce | flops 128 | bytes 1024 | tf_op jit(solution)/shard_map/psum | solution.py:62
  11.9 0.7 dynamic-slice_convert_fusion
  12.6 1.8 fusion.6
  14.4 1.4 convolution_convert_fusion
  15.9 107.5 %all-gather.3.cloned.1.call-done = bf16[16384,1024]{1,0:T(8,128)(2,1)} async-done(((bf16[128,1024]{1,0:T(8,128)(2,1)}), bf16[16384,1024]{1,0:T(8,128)(2,1)}) %all-gather.3.cloned.1.call-update) | async-done | bytes 33554448 | tf_op jit(solution)/shard_map/all_gather | solution.py:66
  123.4 18.8 %fusion.36 = (bf16[64,1,128,1024]{3,2,1,0:T(8,128)(2,1)}, bf16[64,1,128,1024]{3,2,1,0:T(8,128)(2,1)S(1)}) fusion(bf16[64,2,128,1024]{3,2,1,0:T(8,128)(2,1)} %bitcast.39), kind=kLoop, calls=%fused_computation.58 | loop fusion | bytes 67108864 | tf_op jit(solution)/shard_map/slice | solution.py:69
  142.2 5.0 %fusion.12 = f32[8192,224]{0,1:T(8,128)S(1)} fusion(bf16[8192,1024]{1,0:T(8,128)(2,1)S(1)} %bitcast.35, bf16[224,2048]{1,0:T(8,128)(2,1)S(1)} %bitcast.40), kind=kOutput, calls=%fused_computation.17 | convolution fusion | flops 3758096384 | bytes 24576000 | tf_op jit(solution)/shard_map/dot_general | solution.py:40
  147.3 7.2 %fusion.9 = f32[8192,224]{0,1:T(8,128)} fusion(bf16[8192,1024]{1,0:T(8,128)(2,1)S(1)} %bitcast.36, bf16[224,2048]{1,0:T(8,128)(2,1)S(1)} %bitcast.43), kind=kOutput, calls=%fused_computation.14 | convolution fusion | flops 3758096384 | bytes 24576000 | tf_op jit(solution)/shard_map/dot_general | solution.py:40
  154.5 13.9 %convolution_add_fusion.1 = f32[8192,224]{0,1:T(8,128)} fusion(f32[8192,224]{0,1:T(8,128)S(1)} %fusion.12, bf16[8192,1024]{1,0:T(8,128)(2,1)} %bitcast.37, bf16[224,2048]{1,0:T(8,128)(2,1)S(1)} %bitcast.41), kind=kOutput, calls=%fused_computation.2 | convolution fusion | flops 3759931392 | bytes 31916032 | tf_op jit(solution)/shard_map/dot_general | solution.py:40
  168.5 15.5 %fusion.2 = f32[8192,128]{1,0:T(8,128)} fusion(bf16[224,128]{1,0:T(8,128)(2,1)S(1)} %convolution_convert_fusion, f32[8192,224]{0,1:T(8,128)} %fusion.9, bf16[8192,1024]{1,0:T(8,128)(2,1)} %bitcast.38, f32[8192,224]{0,1:T(8,128)} %convolution_add_fusion.1, bf16[224,2048]{1,0:T(8,128)(2,1)S(1)} %bitcast.44), kind=kOutput, calls=%fused_computation.4 | convolution fusion | flops 4240703488 | bytes 36167680 | tf_op jit(solution)/shard_map/dot_general | solution.py:74
  184.0 75.6 %reduce-scatter.2.cloned.1.call-done = f32[512,128]{1,0:T(8,128)} async-done(((f32[8192,128]{1,0:T(8,128)}), f32[512,128]{1,0:T(8,128)}) %reduce-scatter.2.cloned.1.call-update) | async-done | bytes 262160 | tf_op jit(solution)/shard_map/reduce_scatter | solution.py:75
  259.6 4.1 %all-to-all-start = ((f32[4,128,128]{2,1,0:T(8,128)}), f32[4,128,128]{2,1,0:T(8,128)S(1)}, u32[]{:S(2)}, u32[]{:S(2)}) async-start(f32[4,128,128]{2,1,0:T(8,128)} %bitcast.42), calls=%async_computation.1 | async-start | bytes 524288 | tf_op jit(solution)/shard_map/all_to_all | solution.py:77
  263.7 5.5 %all-to-all-done = f32[4,128,128]{2,1,0:T(8,128)S(1)} async-done(((f32[4,128,128]{2,1,0:T(8,128)}), f32[4,128,128]{2,1,0:T(8,128)S(1)}, u32[]{:S(2)}, u32[]{:S(2)}) %all-to-all-start) | async-done | bytes 262176 | tf_op jit(solution)/shard_map/all_to_all | solution.py:77
  269.2 0.8 multiply_reduce_fusion
  270.0 0.1 slice_bitcast_fusion.1
  270.1 0.1 copy.19
  270.2 0.2 reduce-window.7
  270.4 0.1 reduce
  270.5 23.9 %all-reduce.2.cloned.1.call-done = f32[128,128]{1,0:T(8,128)} async-done(((f32[128,128]{1,0:T(8,128)}), f32[128,128]{1,0:T(8,128)}) %all-reduce.2.cloned.1.call-update) | async-done | bytes 65552 | tf_op jit(solution)/shard_map/psum | solution.py:83
  294.4 1.0 select_reduce_fusion
  295.4 0.1 slice_bitcast_fusion
  295.5 0.8 convolution_bitcast_fusion
  296.3 1.5 copy.21
  (29 shorter events, 0.2 us)
Async XLA Ops:
  7.2 7.3 %copy-start = (bf16[1,224,2048]{2,1,0:T(8,128)(2,1)S(1)}, bf16[1,224,2048]{2,1,0:T(8,128)(2,1)}, u32[]{:S(2)}) copy-start(bf16[1,224,2048]{2,1,0:T(8,128)(2,1)} %param.17) | copy-start | bytes 2752516
  7.2 116.3 %all-gather.3.cloned.1.call-start = ((), (), s32[]{:S(2)}) async-start(), calls=%async_computation.4 | async-start | bytes 33816576 | tf_op jit(solution)/shard_map/all_gather | solution.py:66
  14.4 245.2 %reduce-scatter.2.cloned.1.call-start = ((), (), s32[]{:S(2)}) async-start(), calls=%async_computation.2 | async-start | bytes 4456448 | tf_op jit(solution)/shard_map/reduce_scatter | solution.py:75
  123.4 18.8 %copy-start.2 = (bf16[1,224,2048]{2,1,0:T(8,128)(2,1)S(1)}, bf16[1,224,2048]{2,1,0:T(8,128)(2,1)}, u32[]{:S(2)}) copy-start(bf16[1,224,2048]{2,1,0:T(8,128)(2,1)} %param.15) | copy-start | bytes 2752516
  142.2 5.1 %copy-start.3 = (bf16[1,224,2048]{2,1,0:T(8,128)(2,1)S(1)}, bf16[1,224,2048]{2,1,0:T(8,128)(2,1)}, u32[]{:S(2)}) copy-start(bf16[1,224,2048]{2,1,0:T(8,128)(2,1)} %param.16) | copy-start | bytes 2752516
  168.4 15.5 %copy-start.4 = (s32[128,2]{0,1:T(2,128)S(1)}, s32[128,2]{0,1:T(2,128)}, u32[]{:S(2)}) copy-start(s32[128,2]{0,1:T(2,128)} %param.14) | copy-start | bytes 3076
  168.4 15.6 %copy-start.5 = (s32[128,2]{0,1:T(2,128)S(1)}, s32[128,2]{0,1:T(2,128)}, u32[]{:S(2)}) copy-start(s32[128,2]{0,1:T(2,128)} %param.13) | copy-start | bytes 3076
  168.4 95.3 %copy-start.7 = (s32[128]{0:T(128)S(1)}, s32[128]{0:T(128)}, u32[]{:S(2)}) copy-start(s32[128]{0:T(128)} %param.21) | copy-start | bytes 1540
  168.4 126.0 %copy-start.6 = (s32[128]{0:T(128)S(1)}, s32[128]{0:T(128)}, u32[]{:S(2)}) copy-start(s32[128]{0:T(128)} %param.19) | copy-start | bytes 1540
  168.4 127.0 %copy-start.8 = (s32[128]{0:T(128)S(1)}, s32[128]{0:T(128)}, u32[]{:S(2)}) copy-start(s32[128]{0:T(128)} %param.20) | copy-start | bytes 1540
  168.4 129.3 %copy-start.1 = (bf16[1,224,2048]{2,1,0:T(8,128)(2,1)S(1)}, bf16[1,224,2048]{2,1,0:T(8,128)(2,1)}, u32[]{:S(2)}) copy-start(bf16[1,224,2048]{2,1,0:T(8,128)(2,1)} %param.17) | copy-start | bytes 2752516
  259.6 9.7 %all-to-all-start = ((f32[4,128,128]{2,1,0:T(8,128)}), f32[4,128,128]{2,1,0:T(8,128)S(1)}, u32[]{:S(2)}, u32[]{:S(2)}) async-start(f32[4,128,128]{2,1,0:T(8,128)} %bitcast.42), calls=%async_computation.1 | async-start | bytes 524288 | tf_op jit(solution)/shard_map/all_to_all | solution.py:77
  263.7 30.7 %all-reduce.2.cloned.1.call-start = ((), (), s32[]{:S(2)}) async-start(), calls=%async_computation.3 | async-start | bytes 131072 | tf_op jit(solution)/shard_map/psum | solution.py:83
Sparse Core Ops, SparseCore 0:
  14.5 108.8 all-gather.2
  184.1 75.4 reduce-scatter.1
  270.1 24.1 all-reduce.1
where the time goes:
time: 305 us; the launch traced here: 304 us
  waiting for transfers between devices  213 us (70%)
  matrix products  43.9 us (14%)
  local copies, waits for them, and re-layouts  20.6 us (7%)
  between operations  13.8 us (5%)
  other arithmetic  5.72 us (2%)
  starting transfers between devices  4.22 us (1%)
  blocking collectives  3.5 us (1%)
    all_gather x1, waiting for transfers between devices, per_device(): everyone = lax.all_gather(normed, ('dp', 'expert', 'tensor'), axis=0)  108 us
    reduce_scatter x1, waiting for transfers between devices, per_device(): value = lax.psum_scatter(value, 'dp', scatter_dimension=0, tiled=True)  75.6 us
    dot_general x3, matrix products, rows_by(): lax.dot_general(a, b, (((1,), (1,)), ((), ())), preferred_element_type=jn...  26.2 us
    psum x1, waiting for transfers between devices, per_device(): action_values = lax.psum(blended, 'tensor')  23.9 us
    slice x1, local copies, waits for them, and re-layouts, per_device(): right = everyone[:, 1].reshape(dp * ex * rows, half)  18.8 us
    dot_general x1, matrix products, per_device(): value = jnp.dot(hidden, folded, preferred_element_type=jnp.float32)  15.5 us
  transfers between devices with their start and end apart: 4, of which 4 were waited for; matrix products, arithmetic and copies ran while one was open for 1% of the time, Pallas kernels for 0%

commit v1 on v0

--- a/solution.py
+++ b/solution.py
@@ -80,7 +80,7 @@
     named = expert_ids[None] == jnp.arange(ex, dtype=jnp.int32)[:, None, None]
     by_expert = jnp.sum(jnp.where(named, share[None], 0.0), axis=2)
     blended = jnp.sum(value * by_expert[:, :, None], axis=0)
-    action_values = lax.psum(blended, "tensor")
+    action_values = jnp.sum(lax.all_gather(blended, "tensor"), axis=0)
     return (action_values, retrace(action_values, actions, rewards, trace_codes))
 
 

time: 305 us -> 283 us (0.928)
  waiting for transfers between devices: 213 us -> 188 us
  blocking collectives: 3.5 us -> 8.93 us
    psum x1 -> x0, waiting for transfers between devices: 23.9 us -> none  [per_device(): action_values = lax.psum(blended, 'tensor')]
    all_gather x0 -> x1, blocking collectives: none -> 5.42 us  [per_device(): action_values = jnp.sum(lax.all_gather(blended, 'tensor'), axis=0)]
  transfers between devices with their start and end apart: 4 -> 3, of which waited for: 4 -> 3; matrix products, arithmetic and copies ran while one was open for 1% -> 1% of each run, Pallas kernels for 0% -> 0%
where the time goes in v1:
time: 283 us
  waiting for transfers between devices  188 us (66%)
  matrix products  43.9 us (16%)
  local copies, waits for them, and re-layouts  19.1 us (7%)
  between operations  14.2 us (5%)
  blocking collectives  8.93 us (3%)
  other arithmetic  4.27 us (2%)
  starting transfers between devices  4.22 us (1%)
    all_gather x1, waiting for transfers between devices, per_device(): everyone = lax.all_gather(normed, ('dp', 'expert', 'tensor'), axis=0)  108 us
    reduce_scatter x1, waiting for transfers between devices, per_device(): value = lax.psum_scatter(value, 'dp', scatter_dimension=0, tiled=True)  75.2 us
    dot_general x3, matrix products, rows_by(): lax.dot_general(a, b, (((1,), (1,)), ((), ())), preferred_element_type=jn...  26.2 us
    slice x1, local copies, waits for them, and re-layouts, per_device(): right = everyone[:, 1].reshape(dp * ex * rows, half)  18.8 us
    dot_general x1, matrix products, per_device(): value = jnp.dot(hidden, folded, preferred_element_type=jnp.float32)  15.5 us
  transfers between devices with their start and end apart: 3, of which 3 were waited for; matrix products, arithmetic and copies ran while one was open for 1% of the time, Pallas kernels for 0%

profile of v1, /device:TPU:1, one launch (start us, length us, event | category | flops | bytes accessed | tf_op | source)
XLA Modules:
  0.0 282.8 jit_solution(2341151903078865495)
XLA Ops:
  7.2 1.2 fusion.4
  8.4 3.5 %psum.7 = f32[128,1]{0,1:T(1,128)S(1)} all-reduce(f32[128,1]{0,1:T(1,128)S(1)} %bitcast.49), channel_id=1, replica_groups=mesh['dp'=16,'expert'=4,'tensor'=2] {'tensor'}, use_global_device_ids=true, to_apply=%region_1.0 | all-reduce | flops 128 | bytes 1024 | tf_op jit(solution)/shard_map/psum | solution.py:62
  11.9 0.7 dynamic-slice_convert_fusion
  12.6 1.8 fusion.6
  14.4 0.0 reduce-scatter.2.cloned.1.call-start
  14.4 1.4 convolution_convert_fusion
  15.9 107.5 %all-gather.4.cloned.1.call-done = bf16[16384,1024]{1,0:T(8,128)(2,1)} async-done(((bf16[128,1024]{1,0:T(8,128)(2,1)}), bf16[16384,1024]{1,0:T(8,128)(2,1)}) %all-gather.4.cloned.1.call-update) | async-done | bytes 33554448 | tf_op jit(solution)/shard_map/all_gather | solution.py:66
  123.4 18.8 %fusion.36 = (bf16[64,1,128,1024]{3,2,1,0:T(8,128)(2,1)}, bf16[64,1,128,1024]{3,2,1,0:T(8,128)(2,1)S(1)}) fusion(bf16[64,2,128,1024]{3,2,1,0:T(8,128)(2,1)} %bitcast.40), kind=kLoop, calls=%fused_computation.58 | loop fusion | bytes 67108864 | tf_op jit(solution)/shard_map/slice | solution.py:69
  142.2 5.0 %fusion.12 = f32[8192,224]{0,1:T(8,128)S(1)} fusion(bf16[8192,1024]{1,0:T(8,128)(2,1)S(1)} %bitcast.36, bf16[224,2048]{1,0:T(8,128)(2,1)S(1)} %bitcast.41), kind=kOutput, calls=%fused_computation.17 | convolution fusion | flops 3758096384 | bytes 24576000 | tf_op jit(solution)/shard_map/dot_general | solution.py:40
  147.3 7.2 %fusion.9 = f32[8192,224]{0,1:T(8,128)} fusion(bf16[8192,1024]{1,0:T(8,128)(2,1)S(1)} %bitcast.37, bf16[224,2048]{1,0:T(8,128)(2,1)S(1)} %bitcast.45), kind=kOutput, calls=%fused_computation.14 | convolution fusion | flops 3758096384 | bytes 24576000 | tf_op jit(solution)/shard_map/dot_general | solution.py:40
  154.5 13.9 %convolution_add_fusion.1 = f32[8192,224]{0,1:T(8,128)} fusion(f32[8192,224]{0,1:T(8,128)S(1)} %fusion.12, bf16[8192,1024]{1,0:T(8,128)(2,1)} %bitcast.38, bf16[224,2048]{1,0:T(8,128)(2,1)S(1)} %bitcast.42), kind=kOutput, calls=%fused_computation.2 | convolution fusion | flops 3759931392 | bytes 31916032 | tf_op jit(solution)/shard_map/dot_general | solution.py:40
  168.5 15.5 %fusion.2 = f32[8192,128]{1,0:T(8,128)} fusion(bf16[224,128]{1,0:T(8,128)(2,1)S(1)} %convolution_convert_fusion, f32[8192,224]{0,1:T(8,128)} %fusion.9, bf16[8192,1024]{1,0:T(8,128)(2,1)} %bitcast.39, f32[8192,224]{0,1:T(8,128)} %convolution_add_fusion.1, bf16[224,2048]{1,0:T(8,128)(2,1)S(1)} %bitcast.46), kind=kOutput, calls=%fused_computation.4 | convolution fusion | flops 4240703488 | bytes 36167680 | tf_op jit(solution)/shard_map/dot_general | solution.py:74
  184.0 0.1 copy.19
  184.1 0.2 reduce-window.7
  184.2 0.1 reduce
  184.4 75.2 %reduce-scatter.2.cloned.1.call-done = f32[512,128]{1,0:T(8,128)} async-done(((f32[8192,128]{1,0:T(8,128)}), f32[512,128]{1,0:T(8,128)}) %reduce-scatter.2.cloned.1.call-update) | async-done | bytes 262160 | tf_op jit(solution)/shard_map/reduce_scatter | solution.py:75
  259.6 4.1 %all-to-all-start = ((f32[4,128,128]{2,1,0:T(8,128)}), f32[4,128,128]{2,1,0:T(8,128)S(1)}, u32[]{:S(2)}, u32[]{:S(2)}) async-start(f32[4,128,128]{2,1,0:T(8,128)} %bitcast.44), calls=%async_computation.1 | async-start | bytes 524288 | tf_op jit(solution)/shard_map/all_to_all | solution.py:77
  263.7 0.1 slice_bitcast_fusion.1
  263.8 5.5 %all-to-all-done = f32[4,128,128]{2,1,0:T(8,128)S(1)} async-done(((f32[4,128,128]{2,1,0:T(8,128)}), f32[4,128,128]{2,1,0:T(8,128)S(1)}, u32[]{:S(2)}, u32[]{:S(2)}) %all-to-all-start) | async-done | bytes 262176 | tf_op jit(solution)/shard_map/all_to_all | solution.py:77
  269.2 0.1 multiply_reduce_fusion
  269.4 5.4 %all-gather.1 = f32[256,128]{1,0:T(8,128)S(1)} all-gather(f32[128,128]{1,0:T(8,128)S(1)} %multiply_reduce_fusion), channel_id=3, replica_groups=mesh['dp'=16,'expert'=4,'tensor'=2] {'tensor'}, dimensions={0}, use_global_device_ids=true | all-gather | bytes 196608 | tf_op jit(solution)/shard_map/all_gather | solution.py:83
  274.8 0.2 select_reduce_fusion
  275.0 0.1 slice_bitcast_fusion
  275.1 0.8 convolution_bitcast_fusion
  (29 shorter events, 0.2 us)
Async XLA Ops:
  7.2 7.3 %copy-start = (bf16[1,224,2048]{2,1,0:T(8,128)(2,1)S(1)}, bf16[1,224,2048]{2,1,0:T(8,128)(2,1)}, u32[]{:S(2)}) copy-start(bf16[1,224,2048]{2,1,0:T(8,128)(2,1)} %param.17) | copy-start | bytes 2752516
  7.2 116.3 %all-gather.4.cloned.1.call-start = ((), (), s32[]{:S(2)}) async-start(), calls=%async_computation.3 | async-start | bytes 33816576 | tf_op jit(solution)/shard_map/all_gather | solution.py:66
  14.4 245.2 %reduce-scatter.2.cloned.1.call-start = ((), (), s32[]{:S(2)}) async-start(), calls=%async_computation.2 | async-start | bytes 4456448 | tf_op jit(solution)/shard_map/reduce_scatter | solution.py:75
  123.4 18.8 %copy-start.2 = (bf16[1,224,2048]{2,1,0:T(8,128)(2,1)S(1)}, bf16[1,224,2048]{2,1,0:T(8,128)(2,1)}, u32[]{:S(2)}) copy-start(bf16[1,224,2048]{2,1,0:T(8,128)(2,1)} %param.15) | copy-start | bytes 2752516
  142.2 5.1 %copy-start.4 = (bf16[1,224,2048]{2,1,0:T(8,128)(2,1)S(1)}, bf16[1,224,2048]{2,1,0:T(8,128)(2,1)}, u32[]{:S(2)}) copy-start(bf16[1,224,2048]{2,1,0:T(8,128)(2,1)} %param.16) | copy-start | bytes 2752516
  168.4 15.5 %copy-start.8 = (s32[128]{0:T(128)S(1)}, s32[128]{0:T(128)}, u32[]{:S(2)}) copy-start(s32[128]{0:T(128)} %param.21) | copy-start | bytes 1540
  168.4 15.9 %copy-start.5 = (s32[128,2]{0,1:T(2,128)S(1)}, s32[128,2]{0,1:T(2,128)}, u32[]{:S(2)}) copy-start(s32[128,2]{0,1:T(2,128)} %param.14) | copy-start | bytes 3076
  168.4 16.0 %copy-start.6 = (s32[128,2]{0,1:T(2,128)S(1)}, s32[128,2]{0,1:T(2,128)}, u32[]{:S(2)}) copy-start(s32[128,2]{0,1:T(2,128)} %param.13) | copy-start | bytes 3076
  168.4 106.4 %copy-start.7 = (s32[128]{0:T(128)S(1)}, s32[128]{0:T(128)}, u32[]{:S(2)}) copy-start(s32[128]{0:T(128)} %param.19) | copy-start | bytes 1540
  168.4 106.7 %copy-start.9 = (s32[128]{0:T(128)S(1)}, s32[128]{0:T(128)}, u32[]{:S(2)}) copy-start(s32[128]{0:T(128)} %param.20) | copy-start | bytes 1540
  168.4 107.5 %copy-start.1 = (bf16[1,224,2048]{2,1,0:T(8,128)(2,1)S(1)}, bf16[1,224,2048]{2,1,0:T(8,128)(2,1)}, u32[]{:S(2)}) copy-start(bf16[1,224,2048]{2,1,0:T(8,128)(2,1)} %param.17) | copy-start | bytes 2752516
  259.6 9.7 %all-to-all-start = ((f32[4,128,128]{2,1,0:T(8,128)}), f32[4,128,128]{2,1,0:T(8,128)S(1)}, u32[]{:S(2)}, u32[]{:S(2)}) async-start(f32[4,128,128]{2,1,0:T(8,128)} %bitcast.44), calls=%async_computation.1 | async-start | bytes 524288 | tf_op jit(solution)/shard_map/all_to_all | solution.py:77
  274.8 1.1 copy-start.3
Sparse Core Ops, SparseCore 0:
  14.5 108.8 all-gather.3
  184.1 75.4 reduce-scatter.1
